TPU v7x, 32 devices: a whole 2x2x4 slice. The times are simulated.
32 devices in a mesh: dp: 2 (over x), expert: 16 (over z, y, core).
Axes of the slice: x: 2, y: 2, z: 4, core: 2. Of those that a mesh axis runs over, the one named last changes fastest.
Arguments:
- tokens: bfloat16 [4096, 2048], P(('dp', 'expert')), may hold values from -160 to 160
- router_weight: bfloat16 [2048, 16], replicated, may hold values from -0.25 to 0.25
- route_ids: int32 [4096, 2], P(('dp', 'expert')), may hold values from 0 to 15, as said below
- gate_weight: bfloat16 [16, 768, 2048], P('expert', 'dp'), may hold values from -0.125 to 0.125
- up_weight: bfloat16 [16, 768, 2048], P('expert', 'dp'), may hold values from -0.125 to 0.125
- down_weight: bfloat16 [16, 768, 2048], P('expert', 'dp'), may hold values from -0.21875 to 0.21875
Outputs:
- mixture: bfloat16 [4096, 2048], P(('dp', 'expert'))
- z_loss: float32 [], replicated
Inputs may be any that keep to these rules, and one draw needn't show every extreme that they name: `route_ids`: each row names 2 different experts; among the rows of one device no expert is named more than 20 times, and one expert is named exactly 20 times by the rows of every device.
All inputs are finite; a program needn't handle non-finite values.
Results may differ from a plain program's by a relative error of at most 0.0057.
Values may be sent and summed in bfloat16 or wider, within the bound.
No kernel may reach another device: no remote copies, remote signals or barrier semaphores. Data moves between devices by JAX's collectives and lax.ppermute only.
A program may use at most 64 MiB of HBM per device.

v0:
```python
import jax
import jax.numpy as jnp
from jax import lax
from jax.sharding import PartitionSpec as P


def slot_index(route_ids, experts, capacity):
    flat_ids = route_ids.reshape(-1)
    onehot = (flat_ids[:, None] == jnp.arange(experts, dtype=jnp.int32)[None, :]).astype(jnp.int32)
    before = jnp.cumsum(onehot, axis=0) - onehot
    position = jnp.sum(before * onehot, axis=1)
    return flat_ids * capacity + position


def on_device(tokens, router_weight, route_ids, gate_weight, up_weight, down_weight):
    rows_here, model_width = tokens.shape
    top_count = route_ids.shape[1]
    experts = router_weight.shape[1]
    owners = lax.axis_size("expert")
    local_experts = gate_weight.shape[0]
    capacity = 5 * rows_here * top_count // (4 * experts)
    logits = jnp.dot(tokens, router_weight, preferred_element_type=jnp.float32)
    log_total = jax.nn.logsumexp(logits, axis=1)
    local_sum = jnp.sum(log_total * log_total)
    chosen = jnp.take_along_axis(logits, route_ids, axis=1)
    route_weight = jax.nn.softmax(chosen, axis=1)
    slots = slot_index(route_ids, experts, capacity)
    pair_count = slots.shape[0]
    slot_match = slots[None, :] == jnp.arange(experts * capacity, dtype=jnp.int32)[:, None]
    token_of = jnp.arange(pair_count, dtype=jnp.int32) // top_count
    source_row = jnp.sum(jnp.where(slot_match, token_of[None, :], 0), axis=1)
    filled = jnp.any(slot_match, axis=1)
    dispatch = jnp.where(filled[:, None], tokens[source_row], jnp.zeros((), tokens.dtype))
    dispatch = dispatch.reshape(experts, capacity, model_width)
    received = lax.all_to_all(dispatch, "expert", split_axis=0, concat_axis=0, tiled=True)
    expert_rows = received.reshape(owners, local_experts, capacity, model_width)
    expert_rows = expert_rows.transpose(1, 0, 2, 3).reshape(
        local_experts, owners * capacity, model_width
    )
    gate_piece, up_piece = lax.all_gather((gate_weight, up_weight), "dp", axis=1, tiled=True)
    gate_val = jnp.einsum(
        "erd,efd->erf", expert_rows, gate_piece, preferred_element_type=jnp.float32
    )
    up_val = jnp.einsum("erd,efd->erf", expert_rows, up_piece, preferred_element_type=jnp.float32)
    hidden_all = (jax.nn.silu(gate_val) * up_val).astype(jnp.bfloat16)
    summed = jnp.einsum(
        "erf,efd->erd",
        hidden_all,
        lax.all_gather(down_weight, "dp", axis=1, tiled=True),
        preferred_element_type=jnp.float32,
    )
    expert_out = summed.astype(jnp.bfloat16)
    outgoing = expert_out.reshape(local_experts, owners, capacity, model_width)
    outgoing = outgoing.transpose(1, 0, 2, 3).reshape(experts, capacity, model_width)
    returned = lax.all_to_all(outgoing, "expert", split_axis=0, concat_axis=0, tiled=True)
    flat_rows = returned.reshape(experts * capacity, model_width)
    picked = flat_rows[slots].reshape(rows_here, top_count, model_width)
    mixed_out = jnp.sum(route_weight[:, :, None] * picked.astype(jnp.float32), axis=1).astype(
        jnp.bfloat16
    )
    total_sum = lax.psum(local_sum, ("dp", "expert"))
    token_total = rows_here * lax.axis_size("dp") * owners
    z_loss = total_sum / jnp.float32(token_total)
    return (mixed_out, z_loss)


def solution(mesh):
    in_specs = (
        P(("dp", "expert"), None),
        P(),
        P(("dp", "expert"), None),
        P("expert", "dp", None),
        P("expert", "dp", None),
        P("expert", "dp", None),
    )
    out_specs = (P(("dp", "expert"), None), P())
    return jax.shard_map(
        on_device, mesh=mesh, in_specs=in_specs, out_specs=out_specs, check_vma=False
    )
```

profile of v0, /device:TPU:13, one launch (start us, length us, event | category | flops | bytes accessed | tf_op | source)
XLA Modules:
  0.0 237.4 jit_solution(12554654109535446574)
XLA Ops:
  7.2 0.7 all-gather.4.cloned.1.call-update
  8.0 0.7 all-gather.6.cloned.1.call-update
  8.7 0.7 all-gather.8.cloned.1.call-update
  9.5 0.1 eq.39
  9.7 0.1 reshape.163
  9.8 0.6 reduce-window.6
  10.4 0.2 slice_reduce_fusion
  10.7 0.2 fusion.18
  10.9 0.1 select_reduce_fusion
  11.1 2.4 %gather_fusion = bf16[320,2048]{1,0:T(8,128)(2,1)S(1)} fusion(bf16[128,2048]{1,0:T(8,128)(2,1)S(1)} %copy-done, s32[1024]{0:T(1024)S(1)} %pad_clamp_fusion.1), kind=kCustom, calls=%fused_computation | custom fusion | bytes 2622720 | tf_op jit(solution)/shard_map/gather | solution.py:33
  13.5 0.3 gather.14
  14.0 0.2 broadcast_select_fusion
  14.2 42.4 %all_to_all.10 = bf16[16,20,2048]{2,1,0:T(8,128)(2,1)S(1)} all-to-all(bf16[16,20,2048]{2,1,0:T(8,128)(2,1)S(1)} %broadcast_select_fusion), channel_id=1, replica_groups=mesh['dp'=2,'expert'=16] {'expert'}, dimensions={0} | all-to-all | bytes 2621440 | tf_op jit(solution)/shard_map/all_to_all | solution.py:35
  56.5 0.3 reshape.165
  56.8 4.1 %fusion.4 = f32[320,768]{1,0:T(8,128)} fusion(bf16[320,2048]{1,0:T(8,128)(2,1)S(1)} %reshape.165, bf16[1,768,2048]{2,1,0:T(8,128)(2,1)} %all-gather.4.cloned.1.call-done), kind=kOutput, calls=%fused_computation.7 | convolution fusion | flops 1006632960 | bytes 5439488 | tf_op jit(solution)/shard_map/erd,efd->erf/dot_general | solution.py:41
  60.9 41.0 %all-gather.6.cloned.1.call-done = bf16[1,768,2048]{2,1,0:T(8,128)(2,1)} async-done(((bf16[1,384,2048]{2,1,0:T(8,128)(2,1)}), bf16[1,768,2048]{2,1,0:T(8,128)(2,1)}) %all-gather.6.cloned.1.call-update) | async-done | bytes 3145744 | tf_op jit(solution)/shard_map/all_gather | solution.py:40
  101.9 46.5 %all-gather.8.cloned.1.call-done = bf16[1,768,2048]{2,1,0:T(8,128)(2,1)} async-done(((bf16[1,384,2048]{2,1,0:T(8,128)(2,1)}), bf16[1,768,2048]{2,1,0:T(8,128)(2,1)}) %all-gather.8.cloned.1.call-update) | async-done | bytes 3145744 | tf_op jit(solution)/shard_map/all_gather | solution.py:49
  148.4 5.8 %fusion.6 = bf16[320,2048]{1,0:T(8,128)(2,1)S(1)} fusion(bf16[1,768,2048]{2,1,0:T(8,128)(2,1)} %all-gather.8.cloned.1.call-done, bf16[320,2048]{1,0:T(8,128)(2,1)S(1)} %reshape.165, bf16[1,768,2048]{2,1,0:T(8,128)(2,1)} %all-gather.6.cloned.1.call-done, f32[320,768]{1,0:T(8,128)} %fusion.4), kind=kOutput, calls=%fused_computation.9 | convolution fusion | flops 2015395840 | bytes 9895936 | tf_op jit(solution)/shard_map/erf,efd->erd/dot_general | solution.py:46
  154.2 1.3 reshape_transpose_reshape.4
  155.5 6.6 %all-to-all-start.1 = ((bf16[16,20,2048]{2,1,0:T(8,128)(2,1)}), bf16[16,20,2048]{2,1,0:T(8,128)(2,1)S(1)}, u32[]{:S(2)}, u32[]{:S(2)}) async-start(bf16[16,20,2048]{2,1,0:T(8,128)(2,1)} %reshape_transpose_reshape.4), calls=%async_computation.1 | async-start | bytes 3145728 | tf_op jit(solution)/shard_map/all_to_all | solution.py:55
  162.1 0.3 fusion.28
  162.4 0.6 multiply_reduce_fusion.1
  163.0 54.1 %psum.7 = f32[]{:T(128)} all-reduce(f32[]{:T(128)} %multiply_reduce_fusion.1), channel_id=1, replica_groups=mesh['dp'=2,'expert'=16] {'dp','expert'}, use_global_device_ids=true, to_apply=%region_11.12 | all-reduce | flops 1 | bytes 8 | tf_op jit(solution)/shard_map/psum | solution.py:61
  217.2 0.1 copy.33
  217.3 0.1 mul.55
  217.5 0.1 reshape.187
  217.7 2.0 gather_fusion.2
  219.7 0.1 reshape.190
  220.8 0.3 reshape.169
  221.1 2.3 gather_fusion.1
  223.4 2.4 reshape.170
  225.8 3.9 %multiply_reduce_fusion = bf16[128,2048]{1,0:T(8,128)(2,1)} fusion(f32[128,2,2048]{2,1,0:T(2,128)S(1)} %reshape.170, f32[128,2]{1,0:T(8,128)S(1)} %copy.29), kind=kLoop, calls=%fused_computation.10 | loop fusion | flops 786432 | bytes 2622464 | tf_op jit(solution)/shard_map/reduce_sum | solution.py:58
  (32 shorter events, 0.9 us)
Async XLA Ops:
  7.2 3.9 %copy-start = (bf16[128,2048]{1,0:T(8,128)(2,1)S(1)}, bf16[128,2048]{1,0:T(8,128)(2,1)}, u32[]{:S(2)}) copy-start(bf16[128,2048]{1,0:T(8,128)(2,1)} %param.6) | copy-start | bytes 1572868
  7.2 49.7 %all-gather.4.cloned.1.call-start = ((), (), s32[]{:S(2)}) async-start(), calls=%async_computation.2 | async-start | bytes 4718592 | tf_op jit(solution)/shard_map/all_gather | solution.py:40
  7.9 1.5 copy-start.2
  7.9 94.0 %all-gather.6.cloned.1.call-start = ((), (), s32[]{:S(2)}) async-start(), calls=%async_computation.3 | async-start | bytes 4718592 | tf_op jit(solution)/shard_map/all_gather | solution.py:40
  8.7 139.7 %all-gather.8.cloned.1.call-start = ((), (), s32[]{:S(2)}) async-start(), calls=%async_computation.4 | async-start | bytes 4718592 | tf_op jit(solution)/shard_map/all_gather | solution.py:49
  155.5 6.6 %copy-start.1 = (bf16[2048,16]{0,1:T(8,128)(2,1)S(1)}, bf16[2048,16]{0,1:T(8,128)(2,1)}, u32[]{:S(2)}) copy-start(bf16[2048,16]{0,1:T(8,128)(2,1)} %param.7) | copy-start | bytes 196612
  155.5 65.3 %all-to-all-start.1 = ((bf16[16,20,2048]{2,1,0:T(8,128)(2,1)}), bf16[16,20,2048]{2,1,0:T(8,128)(2,1)S(1)}, u32[]{:S(2)}, u32[]{:S(2)}) async-start(bf16[16,20,2048]{2,1,0:T(8,128)(2,1)} %reshape_transpose_reshape.4), calls=%async_computation.1 | async-start | bytes 3145728 | tf_op jit(solution)/shard_map/all_to_all | solution.py:55
Sparse Core Ops, SparseCore 0:
  9.5 45.8 all-gather.3
  57.0 44.8 all-gather.5
  103.5 44.8 all-gather.7
where the time goes:
time: 241 us; the launch traced here: 237 us
  blocking collectives  96.5 us (40%)
  waiting for transfers between devices  89.6 us (37%)
  between operations  15.8 us (7%)
  local copies, waits for them, and re-layouts  12.9 us (5%)
  matrix products  10.1 us (4%)
  starting transfers between devices  6.75 us (3%)
  other arithmetic  5.92 us (2%)
    psum x1, blocking collectives, on_device(): total_sum = lax.psum(local_sum, ('dp', 'expert'))  54.1 us
    all_gather x1, waiting for transfers between devices, on_device(): lax.all_gather(down_weight, 'dp', axis=1, tiled=True)  46.5 us
    all_to_all x1, blocking collectives, on_device(): lax.all_to_all(dispatch, 'expert', split_axis=0, concat_axis=0, tiled=True)  42.4 us
    all_gather x2, waiting for transfers between devices, on_device(): lax.all_gather((gate_weight, up_weight), 'dp', axis=1, tiled=True)  41 us
    all_to_all x1, starting transfers between devices, on_device(): lax.all_to_all(outgoing, 'expert', split_axis=0, concat_axis=0, tiled=True)  6.64 us
    dot_general x1, matrix products, on_device(): jnp.einsum('erf,efd->erd', hidden_all, lax.all_gather(down_weight, 'dp',...  5.77 us
  transfers between devices with their start and end apart: 4, of which 2 were waited for; matrix products, arithmetic and copies ran while one was open for 5% of the time, Pallas kernels for 0%

commit v1 on v0

v1 whole, which is shorter than its diff:
```python
import jax
import jax.numpy as jnp
from jax import lax
from jax.sharding import PartitionSpec as P


def column_parts(capacity):
    parts = 1
    while (parts * capacity) % 8:
        parts *= 2
    return parts


def swap_dp(value):
    size = lax.axis_size("dp")
    return [lax.ppermute(value, "dp", [(s, (s + k) % size) for s in range(size)]) for k in range(1, size)]


def return_dp(values):
    size = lax.axis_size("dp")
    return [
        lax.ppermute(v, "dp", [(s, (s - k) % size) for s in range(size)])
        for k, v in enumerate(values, 1)
    ]


def pack(rows, blocks, parts):
    capacity = rows.shape[0] // blocks
    width = rows.shape[1] // parts
    return (
        rows.reshape(blocks, capacity, parts, width)
        .transpose(0, 2, 1, 3)
        .reshape(blocks, parts * capacity, width)
    )


def unpack(packed, parts):
    blocks, tall, width = packed.shape
    capacity = tall // parts
    return (
        packed.reshape(blocks, parts, capacity, width)
        .transpose(0, 2, 1, 3)
        .reshape(blocks * capacity, parts * width)
    )


def on_device(tokens, router_weight, route_ids, gate_weight, up_weight, down_weight):
    rows_here, model_width = tokens.shape
    top_count = route_ids.shape[1]
    experts = router_weight.shape[1]
    owners = lax.axis_size("expert")
    capacity = 5 * rows_here * top_count // (4 * experts)
    parts = column_parts(capacity)
    tall = parts * capacity
    width = model_width // parts
    gate, up, down = gate_weight[0], up_weight[0], down_weight[0]
    down_other = swap_dp(down)

    expert_at = jnp.arange(experts, dtype=jnp.int32)[:, None]
    ids_t = route_ids.T
    routed = ids_t[0][None, :] == expert_at
    for k in range(1, top_count):
        routed = routed | (ids_t[k][None, :] == expert_at)
    earlier = jnp.arange(rows_here)[:, None] < jnp.arange(rows_here)[None, :]
    before = jnp.dot(
        routed.astype(jnp.bfloat16), earlier.astype(jnp.bfloat16), preferred_element_type=jnp.float32
    )
    position = jnp.where(routed, before, -1.0)
    position_wide = jnp.tile(position, (1, parts))
    tall_at = jnp.arange(tall, dtype=jnp.int32)[None, :, None]
    wide_at = jnp.arange(parts * rows_here, dtype=jnp.int32)[None, None, :]
    match = (position_wide[:, None, :] == (tall_at % capacity).astype(jnp.float32)) & (
        tall_at // capacity == wide_at // rows_here
    )
    stacked = jnp.concatenate(
        [tokens[:, p * width : (p + 1) * width] for p in range(parts)], axis=0
    )
    dispatch = jnp.dot(
        match.astype(jnp.bfloat16).reshape(experts * tall, parts * rows_here),
        stacked,
        preferred_element_type=jnp.float32,
    ).astype(jnp.bfloat16)
    received = lax.all_to_all(
        dispatch.reshape(experts, tall, width), "expert", split_axis=0, concat_axis=0, tiled=True
    )
    others = swap_dp(received)

    tokens_late, router_late, received = lax.optimization_barrier((tokens, router_weight, received))
    logits = lax.dot_general(
        router_late, tokens_late, (((0,), (1,)), ((), ())), preferred_element_type=jnp.float32
    )
    log_total = jax.nn.logsumexp(logits, axis=0)
    local_sum = jnp.sum(log_total * log_total)
    total_sum = lax.psum(local_sum, ("dp", "expert"))
    token_total = rows_here * lax.axis_size("dp") * owners
    z_loss = total_sum / jnp.float32(token_total)
    top_logit = jnp.max(jnp.where(routed, logits, -jnp.inf), axis=0, keepdims=True)
    route_exp = jnp.where(routed, jnp.exp(logits - top_logit), 0.0)
    route_weight = route_exp / jnp.sum(route_exp, axis=0, keepdims=True)
    weight_high = lax.reduce_precision(route_weight, 8, 7)
    weight_low = route_weight - weight_high

    def spread(values):
        wide = jnp.tile(values, (1, parts))[:, None, :]
        return jnp.where(match, wide, 0.0).astype(jnp.bfloat16).reshape(experts * tall, parts * rows_here)

    combine = jnp.concatenate([spread(weight_high), spread(weight_low)], axis=1)

    def half_hidden(packed):
        rows = unpack(packed, parts)
        contract = (((1,), (1,)), ((), ()))
        gate_val = lax.dot_general(rows, gate, contract, preferred_element_type=jnp.float32)
        up_val = lax.dot_general(rows, up, contract, preferred_element_type=jnp.float32)
        return (jax.nn.silu(gate_val) * up_val).astype(jnp.bfloat16)

    own_hidden = half_hidden(received)
    z_loss, others, combine, own_hidden = lax.optimization_barrier((z_loss, others, combine, own_hidden))
    back = return_dp([half_hidden(o) for o in others])
    size = lax.axis_size("dp")
    summed = jnp.dot(own_hidden, down, preferred_element_type=jnp.float32)
    for k in range(1, size):
        summed = summed + jnp.dot(back[k - 1], down_other[size - k - 1], preferred_element_type=jnp.float32)
    outgoing = pack(summed.astype(jnp.bfloat16), owners, parts)
    returned = lax.all_to_all(outgoing, "expert", split_axis=0, concat_axis=0, tiled=True)
    mixed = lax.dot_general(
        combine,
        returned.reshape(experts * tall, width),
        (((0,), (0,)), ((), ())),
        preferred_element_type=jnp.float32,
    )
    mixed = jnp.sum(mixed.reshape(2, parts, rows_here, width), axis=0).astype(jnp.bfloat16)
    return jnp.concatenate([mixed[p] for p in range(parts)], axis=1), z_loss


def solution(mesh):
    in_specs = (
        P(("dp", "expert"), None),
        P(),
        P(("dp", "expert"), None),
        P("expert", "dp", None),
        P("expert", "dp", None),
        P("expert", "dp", None),
    )
    out_specs = (P(("dp", "expert"), None), P())
    return jax.shard_map(
        on_device, mesh=mesh, in_specs=in_specs, out_specs=out_specs, check_vma=False
    )
```

time: 241 us -> 177 us (0.73); the launches traced: 237 us -> 177 us
  blocking collectives: 96.5 us -> 61.6 us
  waiting for transfers between devices: 89.6 us -> 63.2 us
  between operations: 15.8 us -> 2.65 us
  starting transfers between devices: 6.75 us -> 18.7 us
  local copies, waits for them, and re-layouts: 12.9 us -> 17 us
  other arithmetic: 5.92 us -> 2.03 us
    all_gather x3 -> x0, waiting for transfers between devices: 87.5 us -> none  [the longest x1 46.5 us: on_device(): lax.all_gather(down_weight, 'dp', axis=1, tiled=True)]
    all_to_all x1 -> x0, blocking collectives: 42.4 us -> none  [on_device(): lax.all_to_all(dispatch, 'expert', split_axis=0, concat_axis=0, tiled=True)]
    all_to_all x0 -> x1, waiting for transfers between devices: none -> 29.8 us  [on_device(): lax.all_to_all(dispatch.reshape(experts, tall, width), 'expert', split_ax...]
    all_to_all x1, waiting for transfers between devices: 0.01 us -> 29.5 us  [on_device(): lax.all_to_all(outgoing, 'expert', split_axis=0, concat_axis=0, tiled=True)]
    gather x8 -> x0, local copies, waits for them, and re-layouts: 7.51 us -> none  [the longest x2 2.75 us: on_device(): tokens[source_row]]
    psum x1, blocking collectives: 54.1 us -> 61.6 us  [on_device(): total_sum = lax.psum(local_sum, ('dp', 'expert'))]
    all_to_all x0 -> x1, starting transfers between devices: none -> 6.65 us  [on_device(): lax.all_to_all(dispatch.reshape(experts, tall, width), 'expert', split_ax...]
    reshape x2 -> x3, local copies, waits for them, and re-layouts: 0.46 us -> 6.06 us  [the longest x2 4.27 us: pack(): rows.reshape(blocks, capacity, parts, width).transpose(0, 2, 1, 3)]
  transfers between devices with their start and end apart: 4 -> 5, of which waited for: 2 -> 3; matrix products, arithmetic and copies ran while one was open for 5% -> 7% of each run, Pallas kernels for 0% -> 0%
where the time goes in v1:
time: 177 us
  waiting for transfers between devices  63.2 us (36%)
  blocking collectives  61.6 us (35%)
  starting transfers between devices  18.7 us (11%)
  local copies, waits for them, and re-layouts  17 us (10%)
  matrix products  11.7 us (7%)
  between operations  2.65 us (1%)
  other arithmetic  2.03 us (1%)
    psum x1, blocking collectives, on_device(): total_sum = lax.psum(local_sum, ('dp', 'expert'))  61.6 us
    all_to_all x1, waiting for transfers between devices, on_device(): lax.all_to_all(dispatch.reshape(experts, tall, width), 'expert', split_ax...  29.8 us
    all_to_all x1, waiting for transfers between devices, on_device(): lax.all_to_all(outgoing, 'expert', split_axis=0, concat_axis=0, tiled=True)  29.5 us
    all_to_all x1, starting transfers between devices, on_device(): lax.all_to_all(outgoing, 'expert', split_axis=0, concat_axis=0, tiled=True)  8.29 us
    all_to_all x1, starting transfers between devices, on_device(): lax.all_to_all(dispatch.reshape(experts, tall, width), 'expert', split_ax...  6.65 us
    reshape x2, local copies, waits for them, and re-layouts, pack(): rows.reshape(blocks, capacity, parts, width).transpose(0, 2, 1, 3)  4.27 us
    transpose x2, local copies, waits for them, and re-layouts, unpack(): return packed.reshape(blocks, parts, capacity, width).transpose(0, 2, 1,...  4.02 us
    ppermute x1, waiting for transfers between devices, return_dp(): lax.ppermute(v, 'dp', [(s, (s - k) % size) for s in range(size)])  3.96 us
  transfers between devices with their start and end apart: 5, of which 3 were waited for; matrix products, arithmetic and copies ran while one was open for 7% of the time, Pallas kernels for 0%

profile of v1, /device:TPU:13, one launch (start us, length us, event | category | flops | bytes accessed | tf_op | source)
XLA Modules:
  0.0 176.9 jit_solution(8266089769076044282)
XLA Ops:
  0.7 0.8 slice_bitcast_fusion.3
  1.7 1.1 fusion.35
  3.1 1.6 convolution_convert_fusion
  4.7 6.7 %all-to-all-start = ((bf16[16,40,1024]{2,1,0:T(8,128)(2,1)}), bf16[16,40,1024]{2,1,0:T(8,128)(2,1)S(1)}, u32[]{:S(2)}, u32[]{:S(2)}) async-start(bf16[16,40,1024]{2,1,0:T(8,128)(2,1)} %bitcast.97), calls=%async_computation | async-start | bytes 2621440 | tf_op jit(solution)/shard_map/all_to_all | solution.py:83
  11.3 1.2 collective-permute-start.2
  12.5 29.8 %all-to-all-done = bf16[16,40,1024]{2,1,0:T(8,128)(2,1)S(1)} async-done(((bf16[16,40,1024]{2,1,0:T(8,128)(2,1)}), bf16[16,40,1024]{2,1,0:T(8,128)(2,1)S(1)}, u32[]{:S(2)}, u32[]{:S(2)}) %all-to-all-start) | async-done | bytes 1310752 | tf_op jit(solution)/shard_map/all_to_all | solution.py:83
  42.6 1.8 %copy.17 = bf16[16,40,1024]{2,0,1:T(8,128)(2,1)} copy(bf16[16,40,1024]{2,1,0:T(8,128)(2,1)S(1)} %all-to-all-done) | data formatting | bytes 2621440 | tf_op jit(solution)/shard_map/all_to_all | solution.py:83
  44.4 1.2 collective-permute-start
  45.9 0.6 multiply_reduce_fusion
  46.5 61.6 %psum.7 = f32[]{:T(128)} all-reduce(f32[]{:T(128)} %multiply_reduce_fusion), channel_id=1, replica_groups=mesh['dp'=2,'expert'=16] {'dp','expert'}, use_global_device_ids=true, to_apply=%region_3.4 | all-reduce | flops 1 | bytes 8 | tf_op jit(solution)/shard_map/psum | solution.py:94
  108.1 0.7 copy.18
  108.9 1.3 copy.19
  110.2 0.4 copy.29
  111.3 0.9 fusion.7
  112.1 0.5 copy-done.4
  112.7 0.9 fusion.18
  113.5 2.7 %copy.20 = bf16[16,20,2,1024]{3,2,1,0:T(2,128)(2,1)S(1)} copy(bf16[16,20,2,1024]{3,0,1,2:T(8,128)(2,1)} %bitcast.16) | data formatting | bytes 2621440 | tf_op jit(solution)/shard_map/transpose | solution.py:42
  116.2 0.3 copy.30
  116.6 0.9 fusion.5
  117.4 0.9 fusion.15
  118.3 1.4 collective-permute-start.1
  119.7 4.0 %collective-permute-done.1 = bf16[320,384]{1,0:T(8,128)(2,1)S(1)} collective-permute-done((bf16[320,384]{1,0:T(8,128)(2,1)S(1)}, bf16[320,384]{1,0:T(8,128)(2,1)S(1)}, u32[]{:S(2)}, u32[]{:S(2)}) %collective-permute-start.1) | collective-permute-done | bytes 245792 | tf_op jit(solution)/shard_map/ppermute | solution.py:22
  123.7 2.2 %fusion.36 = f32[320,2048]{1,0:T(8,128)S(1)} fusion(bf16[320,384]{1,0:T(8,128)(2,1)S(1)} %collective-permute-done.1, bf16[384,2048]{1,0:T(8,128)(2,1)} %collective-permute-done.2), kind=kOutput, calls=%fused_computation.62 | convolution fusion | flops 503316480 | bytes 4440064 | tf_op jit(solution)/shard_map/dot_general | solution.py:122
  125.9 1.9 %fusion = bf16[320,2048]{1,0:T(8,128)(2,1)} fusion(f32[320,2048]{1,0:T(8,128)S(1)} %fusion.36, bf16[320,384]{1,0:T(8,128)(2,1)S(1)} %fusion.18, bf16[1,384,2048]{2,1,0:T(8,128)(2,1)S(1)} %copy-done.2), kind=kOutput, calls=%fused_computation.1 | convolution fusion | flops 504627200 | bytes 5750784 | tf_op jit(solution)/shard_map/dot_general | solution.py:120
  127.9 3.6 %reshape.179 = bf16[16,20,2,1024]{3,2,1,0:T(2,128)(2,1)S(1)} reshape(bf16[320,2048]{1,0:T(8,128)(2,1)} %fusion) | data formatting | bytes 2621440 | tf_op jit(solution)/shard_map/reshape | solution.py:31
  131.4 0.7 copy.21
  132.1 1.8 %copy.22 = bf16[16,40,1024]{2,1,0:T(8,128)(2,1)} copy(bf16[16,40,1024]{2,0,1:T(8,128)(2,1)S(1)} %bitcast.101) | data formatting | bytes 2621440 | tf_op jit(solution)/shard_map/reshape | solution.py:33
  133.9 8.3 %all-to-all-start.1 = ((bf16[16,40,1024]{2,1,0:T(8,128)(2,1)}), bf16[16,40,1024]{2,1,0:T(8,128)(2,1)S(1)}, u32[]{:S(2)}, u32[]{:S(2)}) async-start(bf16[16,40,1024]{2,1,0:T(8,128)(2,1)} %copy.22), calls=%async_computation.1 | async-start | bytes 2621440 | tf_op jit(solution)/shard_map/all_to_all | solution.py:124
  142.2 1.1 copy.25
  143.3 29.5 %all-to-all-done.1 = bf16[16,40,1024]{2,1,0:T(8,128)(2,1)S(1)} async-done(((bf16[16,40,1024]{2,1,0:T(8,128)(2,1)}), bf16[16,40,1024]{2,1,0:T(8,128)(2,1)S(1)}, u32[]{:S(2)}, u32[]{:S(2)}) %all-to-all-start.1) | async-done | bytes 1310752 | tf_op jit(solution)/shard_map/all_to_all | solution.py:124
  172.8 2.1 %convolution_reduce_fusion = bf16[2,128,1024]{2,1,0:T(8,128)(2,1)S(1)} fusion(bf16[2,2,128,640]{3,2,1,0:T(8,128)(2,1)} %bitcast.109, bf16[640,1024,1,1]{1,0,3,2:T(8,128)(2,1)S(1)} %bitcast.104), kind=kOutput, calls=%fused_computation.11 | convolution fusion | flops 671350784 | bytes 2490368 | tf_op jit(solution)/shard_map/dot_general | solution.py:125
  174.9 0.8 pad_maximum_fusion.1
  (31 shorter events, 1.2 us)
Async XLA Ops:
  0.6 110.6 %copy-start = (bf16[1,384,2048]{2,1,0:T(8,128)(2,1)S(1)}, bf16[1,384,2048]{2,1,0:T(8,128)(2,1)}, u32[]{:S(2)}) copy-start(bf16[1,384,2048]{2,1,0:T(8,128)(2,1)} %param.9) | copy-start | bytes 4718596
  4.7 37.6 %copy-start.1 = (bf16[128,2048]{1,0:T(8,128)(2,1)S(1)}, bf16[128,2048]{1,0:T(8,128)(2,1)}, u32[]{:S(2)}) copy-start(bf16[128,2048]{1,0:T(8,128)(2,1)} %param.6) | copy-start | bytes 1572868
  4.7 37.6 %copy-start.3 = (bf16[2048,16]{0,1:T(8,128)(2,1)S(1)}, bf16[2048,16]{0,1:T(8,128)(2,1)}, u32[]{:S(2)}) copy-start(bf16[2048,16]{0,1:T(8,128)(2,1)} %param.7) | copy-start | bytes 196612
  4.7 37.6 %all-to-all-start = ((bf16[16,40,1024]{2,1,0:T(8,128)(2,1)}), bf16[16,40,1024]{2,1,0:T(8,128)(2,1)S(1)}, u32[]{:S(2)}, u32[]{:S(2)}) async-start(bf16[16,40,1024]{2,1,0:T(8,128)(2,1)} %bitcast.97), calls=%async_computation | async-start | bytes 2621440 | tf_op jit(solution)/shard_map/all_to_all | solution.py:83
  11.3 108.4 %collective-permute-start.2 = (bf16[384,2048]{1,0:T(8,128)(2,1)}, bf16[384,2048]{1,0:T(8,128)(2,1)}, u32[]{:S(2)}, u32[]{:S(2)}) collective-permute-start(bf16[384,2048]{1,0:T(8,128)(2,1)} %bitcast.103), channel_id=1, source_target_pairs={{0,16},{16,0},{1,17},{17,1},{2,18},{18,2},{3,19},{19,3},{4,20},{20... | collective-permute-start | bytes 4718600 | tf_op jit(solution)/shard_map/ppermute | solution.py:16
  44.4 69.2 %collective-permute-start = (bf16[16,40,1024]{2,0,1:T(8,128)(2,1)}, bf16[16,40,1024]{2,0,1:T(8,128)(2,1)}, u32[]{:S(2)}, u32[]{:S(2)}) collective-permute-start(bf16[16,40,1024]{2,0,1:T(8,128)(2,1)} %copy.17), channel_id=1, source_target_pairs={{0,16},{16,0},{1,17},{17,1},{2,18},{18,2},{3,19},{19,3},{4,20},{20... | collective-permute-start | bytes 3932168 | tf_op jit(solution)/shard_map/ppermute | solution.py:16
  111.2 1.4 copy-start.4
  118.3 7.6 %copy-start.2 = (bf16[1,384,2048]{2,1,0:T(8,128)(2,1)S(1)}, bf16[1,384,2048]{2,1,0:T(8,128)(2,1)}, u32[]{:S(2)}) copy-start(bf16[1,384,2048]{2,1,0:T(8,128)(2,1)} %param.11) | copy-start | bytes 4718596
  118.3 5.3 %collective-permute-start.1 = (bf16[320,384]{1,0:T(8,128)(2,1)S(1)}, bf16[320,384]{1,0:T(8,128)(2,1)S(1)}, u32[]{:S(2)}, u32[]{:S(2)}) collective-permute-start(bf16[320,384]{1,0:T(8,128)(2,1)S(1)} %fusion.15), channel_id=1, source_target_pairs={{0,16},{16,0},{1,17},{17,1},{2,18},{18,2},{3,19},{19,3},{4,20},{20... | collective-permute-start | bytes 737288 | tf_op jit(solution)/shard_map/ppermute | solution.py:22
  133.9 38.9 %all-to-all-start.1 = ((bf16[16,40,1024]{2,1,0:T(8,128)(2,1)}), bf16[16,40,1024]{2,1,0:T(8,128)(2,1)S(1)}, u32[]{:S(2)}, u32[]{:S(2)}) async-start(bf16[16,40,1024]{2,1,0:T(8,128)(2,1)} %copy.22), calls=%async_computation.1 | async-start | bytes 2621440 | tf_op jit(solution)/shard_map/all_to_all | solution.py:124

commit v2 on v1

--- a/solution.py
+++ b/solution.py
@@ -24,24 +24,30 @@
     ]
 
 
-def pack(rows, blocks, parts):
-    capacity = rows.shape[0] // blocks
-    width = rows.shape[1] // parts
-    return (
-        rows.reshape(blocks, capacity, parts, width)
-        .transpose(0, 2, 1, 3)
-        .reshape(blocks, parts * capacity, width)
-    )
+def regroup(blocks, parts, capacity, back):
+    total = blocks * parts * capacity
+    packed_at = jnp.arange(total, dtype=jnp.int32)
+    block = packed_at // (parts * capacity)
+    part = packed_at // capacity % parts
+    target = (part * blocks + block) * capacity + packed_at % capacity
+    flat_at = jnp.arange(total, dtype=jnp.int32)
+    hot = flat_at[None, :] == target[:, None] if back else flat_at[:, None] == target[None, :]
+    return hot.astype(jnp.bfloat16)
 
 
-def unpack(packed, parts):
-    blocks, tall, width = packed.shape
-    capacity = tall // parts
-    return (
-        packed.reshape(blocks, parts, capacity, width)
-        .transpose(0, 2, 1, 3)
-        .reshape(blocks * capacity, parts * width)
-    )
+def exact(hot, rows):
+    return jnp.dot(hot, rows, preferred_element_type=jnp.float32).astype(jnp.bfloat16)
+
+
+def sum_over(value, axis):
+    size = lax.axis_size(axis)
+    if size & (size - 1):
+        return lax.psum(value, axis)
+    step = 1
+    while step < size:
+        value = value + lax.ppermute(value, axis, [(s, s ^ step) for s in range(size)])
+        step *= 2
+    return value
 
 
 def on_device(tokens, router_weight, route_ids, gate_weight, up_weight, down_weight):
@@ -91,9 +97,7 @@
     )
     log_total = jax.nn.logsumexp(logits, axis=0)
     local_sum = jnp.sum(log_total * log_total)
-    total_sum = lax.psum(local_sum, ("dp", "expert"))
-    token_total = rows_here * lax.axis_size("dp") * owners
-    z_loss = total_sum / jnp.float32(token_total)
+    group_sum = sum_over(jnp.full((8, 128), local_sum), "expert")
     top_logit = jnp.max(jnp.where(routed, logits, -jnp.inf), axis=0, keepdims=True)
     route_exp = jnp.where(routed, jnp.exp(logits - top_logit), 0.0)
     route_weight = route_exp / jnp.sum(route_exp, axis=0, keepdims=True)
@@ -106,21 +110,40 @@
 
     combine = jnp.concatenate([spread(weight_high), spread(weight_low)], axis=1)
 
+    to_parts = regroup(owners, parts, capacity, False)
+    to_blocks = regroup(owners, parts, capacity, True)
+    rows_all = owners * capacity
+
     def half_hidden(packed):
-        rows = unpack(packed, parts)
+        stack = exact(to_parts, packed.reshape(owners * tall, width))
+        rows = jnp.concatenate(
+            [stack[p * rows_all : (p + 1) * rows_all] for p in range(parts)], axis=1
+        )
         contract = (((1,), (1,)), ((), ()))
         gate_val = lax.dot_general(rows, gate, contract, preferred_element_type=jnp.float32)
         up_val = lax.dot_general(rows, up, contract, preferred_element_type=jnp.float32)
         return (jax.nn.silu(gate_val) * up_val).astype(jnp.bfloat16)
 
     own_hidden = half_hidden(received)
-    z_loss, others, combine, own_hidden = lax.optimization_barrier((z_loss, others, combine, own_hidden))
+    group_sum, others, combine, own_hidden, to_blocks = lax.optimization_barrier(
+        (group_sum, others, combine, own_hidden, to_blocks)
+    )
     back = return_dp([half_hidden(o) for o in others])
+    total_sum = sum_over(group_sum, "dp")
+    total_sum, back = lax.optimization_barrier((total_sum, back))
+    token_total = rows_here * lax.axis_size("dp") * owners
+    z_loss = total_sum[0, 0] / jnp.float32(token_total)
     size = lax.axis_size("dp")
-    summed = jnp.dot(own_hidden, down, preferred_element_type=jnp.float32)
-    for k in range(1, size):
-        summed = summed + jnp.dot(back[k - 1], down_other[size - k - 1], preferred_element_type=jnp.float32)
-    outgoing = pack(summed.astype(jnp.bfloat16), owners, parts)
+    pieces = []
+    for p in range(parts):
+        cols = slice(p * width, (p + 1) * width)
+        summed = jnp.dot(own_hidden, down[:, cols], preferred_element_type=jnp.float32)
+        for k in range(1, size):
+            summed = summed + jnp.dot(
+                back[k - 1], down_other[size - k - 1][:, cols], preferred_element_type=jnp.float32
+            )
+        pieces.append(summed.astype(jnp.bfloat16))
+    outgoing = exact(to_blocks, jnp.concatenate(pieces, axis=0)).reshape(experts, tall, width)
     returned = lax.all_to_all(outgoing, "expert", split_axis=0, concat_axis=0, tiled=True)
     mixed = lax.dot_general(
         combine,

time: 177 us -> 135 us (0.76)
  blocking collectives: 61.6 us -> 0 us
  waiting for transfers between devices: 63.2 us -> 86.9 us
  local copies, waits for them, and re-layouts: 17 us -> 5.13 us
  matrix products: 11.7 us -> 16.5 us
  other arithmetic: 2.03 us -> 4.48 us
    psum x1 -> x0, blocking collectives: 61.6 us -> none  [on_device(): total_sum = lax.psum(local_sum, ('dp', 'expert'))]
    ppermute x2, waiting for transfers between devices: 0.01 us -> 17.4 us  [swap_dp(): lax.ppermute(value, 'dp', [(s, (s + k) % size) for s in range(size)])]
    ppermute x0 -> x5, waiting for transfers between devices: none -> 12.5 us  [sum_over(): lax.ppermute(value, axis, [(s, s ^ step) for s in range(size)])]
    reshape x3 -> x0, local copies, waits for them, and re-layouts: 6.06 us -> none  [the longest x2 4.27 us: pack(): rows.reshape(blocks, capacity, parts, width).transpose(0, 2, 1, 3)]
    dot_general x2 -> x7, matrix products: 4.18 us -> 8.94 us  [the longest x3 4.65 us: exact(): jnp.dot(hot, rows, preferred_element_type=jnp.float32).astype(jnp.bfloat16)]
    transpose x2 -> x0, local copies, waits for them, and re-layouts: 4.02 us -> none  [unpack(): return packed.reshape(blocks, parts, capacity, width).transpose(0, 2, 1,...]
    ppermute x1, waiting for transfers between devices: 3.96 us -> 0.01 us  [return_dp(): lax.ppermute(v, 'dp', [(s, (s - k) % size) for s in range(size)])]
    all_to_all x1 -> x0, local copies, waits for them, and re-layouts: 1.79 us -> none  [on_device(): lax.all_to_all(dispatch.reshape(experts, tall, width), 'expert', split_ax...]
  transfers between devices with their start and end apart: 5 -> 10, of which waited for: 3 -> 7; matrix products, arithmetic and copies ran while one was open for 7% -> 9% of each run, Pallas kernels for 0% -> 0%
where the time goes in v2:
time: 135 us
  waiting for transfers between devices  86.9 us (64%)
  starting transfers between devices  19 us (14%)
  matrix products  16.5 us (12%)
  local copies, waits for them, and re-layouts  5.13 us (4%)
  other arithmetic  4.48 us (3%)
  between operations  2.72 us (2%)
    all_to_all x1, waiting for transfers between devices, on_device(): lax.all_to_all(dispatch.reshape(experts, tall, width), 'expert', split_ax...  28.6 us
    all_to_all x1, waiting for transfers between devices, on_device(): lax.all_to_all(outgoing, 'expert', split_axis=0, concat_axis=0, tiled=True)  28.3 us
    ppermute x2, waiting for transfers between devices, swap_dp(): lax.ppermute(value, 'dp', [(s, (s + k) % size) for s in range(size)])  17.4 us
    ppermute x5, waiting for transfers between devices, sum_over(): lax.ppermute(value, axis, [(s, s ^ step) for s in range(size)])  12.5 us
    all_to_all x1, starting transfers between devices, on_device(): lax.all_to_all(outgoing, 'expert', split_axis=0, concat_axis=0, tiled=True)  7.3 us
    all_to_all x1, starting transfers between devices, on_device(): lax.all_to_all(dispatch.reshape(experts, tall, width), 'expert', split_ax...  6.65 us
    dot_general x3, matrix products, exact(): jnp.dot(hot, rows, preferred_element_type=jnp.float32).astype(jnp.bfloat16)  4.65 us
    dot_general x2, matrix products, on_device(): jnp.dot(back[k - 1], down_other[size - k - 1][:, cols], preferred_element...  3.26 us
  transfers between devices with their start and end apart: 10, of which 7 were waited for; matrix products, arithmetic and copies ran while one was open for 9% of the time, Pallas kernels for 0%

profile of v2, /device:TPU:13, one launch (start us, length us, event | category | flops | bytes accessed | tf_op | source)
XLA Modules:
  0.0 134.6 jit_solution(6352663434512278740)
XLA Ops:
  0.7 0.8 slice_bitcast_fusion.3
  1.7 1.1 fusion.72
  3.1 1.6 %convolution_convert_fusion = bf16[640,1024]{1,0:T(8,128)(2,1)} fusion(pred[640,256]{1,0:T(32,128)(4,1)S(1)} %fusion.40, bf16[128,1024]{1,0:T(8,128)(2,1)S(1)} %get-tuple-element.33, bf16[128,1024]{1,0:T(8,128)(2,1)S(1)} %get-tuple-element.32), kind=kOutput, calls=%fused_computation.7 | convolution fusion | flops 337248256 | bytes 1998848 | tf_op jit(solution)/shard_map/dot_general | solution.py:84
  4.6 6.7 %all-to-all-start = ((bf16[16,40,1024]{2,1,0:T(8,128)(2,1)}), bf16[16,40,1024]{2,1,0:T(8,128)(2,1)S(1)}, u32[]{:S(2)}, u32[]{:S(2)}) async-start(bf16[16,40,1024]{2,1,0:T(8,128)(2,1)} %bitcast.5), calls=%async_computation | async-start | bytes 2621440 | tf_op jit(solution)/shard_map/all_to_all | solution.py:89
  11.3 1.2 collective-permute-start.7
  12.5 1.1 fusion.2
  13.6 28.6 %all-to-all-done = bf16[16,40,1024]{2,1,0:T(8,128)(2,1)S(1)} async-done(((bf16[16,40,1024]{2,1,0:T(8,128)(2,1)}), bf16[16,40,1024]{2,1,0:T(8,128)(2,1)S(1)}, u32[]{:S(2)}, u32[]{:S(2)}) %all-to-all-start) | async-done | bytes 1310752 | tf_op jit(solution)/shard_map/all_to_all | solution.py:89
  43.2 0.6 broadcast_in_dim.52
  43.9 1.2 fusion.3
  45.2 0.9 fusion.11
  46.1 1.3 collective-permute-start.4
  47.4 0.9 fusion.27
  48.3 0.7 broadcast_add_fusion
  49.0 2.7 %collective-permute-done.1 = f32[8,128]{1,0:T(8,128)S(1)} collective-permute-done((f32[8,128]{1,0:T(8,128)S(1)}, f32[8,128]{1,0:T(8,128)S(1)}, u32[]{:S(2)}, u32[]{:S(2)}) %collective-permute-start.1) | collective-permute-done | bytes 4128 | tf_op jit(solution)/shard_map/ppermute | solution.py:48
  51.7 0.6 fusion.85
  52.8 2.5 %collective-permute-done.2 = f32[8,128]{1,0:T(8,128)S(1)} collective-permute-done((f32[8,128]{1,0:T(8,128)S(1)}, f32[8,128]{1,0:T(8,128)S(1)}, u32[]{:S(2)}, u32[]{:S(2)}) %collective-permute-start.2) | collective-permute-done | bytes 4128 | tf_op jit(solution)/shard_map/ppermute | solution.py:48
  55.2 0.8 collective-permute-start.3
  56.1 2.5 %collective-permute-done.3 = f32[8,128]{1,0:T(8,128)S(1)} collective-permute-done((f32[8,128]{1,0:T(8,128)S(1)}, f32[8,128]{1,0:T(8,128)S(1)}, u32[]{:S(2)}, u32[]{:S(2)}) %collective-permute-start.3) | collective-permute-done | bytes 4128 | tf_op jit(solution)/shard_map/ppermute | solution.py:48
  58.6 17.4 %collective-permute-done.4 = bf16[16,40,1024]{2,1,0:T(8,128)(2,1)S(1)} collective-permute-done((bf16[16,40,1024]{2,1,0:T(8,128)(2,1)S(1)}, bf16[16,40,1024]{2,1,0:T(8,128)(2,1)S(1)}, u32[]{:S(2)}, u32[]{:S(2)}) %collective-permute-start.4) | collective-permute-done | bytes 1310752 | tf_op jit(solution)/shard_map/ppermute | solution.py:16
  76.0 1.2 fusion.4
  77.3 0.9 fusion.9
  78.2 0.9 fusion.24
  79.1 1.3 collective-permute-start.6
  80.6 4.8 %collective-permute-done.5 = f32[8,128]{1,0:T(8,128)S(1)} collective-permute-done((f32[8,128]{1,0:T(8,128)S(1)}, f32[8,128]{1,0:T(8,128)S(1)}, u32[]{:S(2)}, u32[]{:S(2)}) %collective-permute-start.5) | collective-permute-done | bytes 4128 | tf_op jit(solution)/shard_map/ppermute | solution.py:48
  85.4 1.6 %fusion.32 = f32[320,1024]{1,0:T(8,128)S(1)} fusion(bf16[320,384]{1,0:T(8,128)(2,1)S(1)} %collective-permute-done.6, bf16[384,2048]{1,0:T(8,128)(2,1)} %collective-permute-done.7), kind=kOutput, calls=%fused_computation.34 | convolution fusion | flops 251658240 | bytes 2342912 | tf_op jit(solution)/shard_map/dot_general | solution.py:142
  87.6 1.6 %fusion.35 = f32[320,1024]{1,0:T(8,128)S(1)} fusion(bf16[320,384]{1,0:T(8,128)(2,1)S(1)} %collective-permute-done.6, bf16[384,2048]{1,0:T(8,128)(2,1)} %collective-permute-done.7), kind=kOutput, calls=%fused_computation.37 | convolution fusion | flops 251658240 | bytes 2342912 | tf_op jit(solution)/shard_map/dot_general | solution.py:142
  90.4 2.3 %convolution_convert_fusion.1 = bf16[640,1024]{1,0:T(8,128)(2,1)} fusion(bf16[640,640]{1,0:T(8,128)(2,1)S(1)} %copy-done.3, bf16[320,1024]{1,0:T(8,128)(2,1)S(1)} %fusion.14, bf16[320,1024]{1,0:T(8,128)(2,1)S(1)} %fusion.13), kind=kOutput, calls=%fused_computation.8 | convolution fusion | flops 842137600 | bytes 3440640 | tf_op jit(solution)/shard_map/dot_general | solution.py:39
  92.6 7.3 %all-to-all-start.1 = ((bf16[16,40,1024]{2,1,0:T(8,128)(2,1)}), bf16[16,40,1024]{2,1,0:T(8,128)(2,1)S(1)}, u32[]{:S(2)}, u32[]{:S(2)}) async-start(bf16[16,40,1024]{2,1,0:T(8,128)(2,1)} %bitcast.90), calls=%async_computation.1 | async-start | bytes 2621440 | tf_op jit(solution)/shard_map/all_to_all | solution.py:147
  99.9 1.1 copy.13
  102.2 28.3 %all-to-all-done.1 = bf16[16,40,1024]{2,1,0:T(8,128)(2,1)S(1)} async-done(((bf16[16,40,1024]{2,1,0:T(8,128)(2,1)}), bf16[16,40,1024]{2,1,0:T(8,128)(2,1)S(1)}, u32[]{:S(2)}, u32[]{:S(2)}) %all-to-all-start.1) | async-done | bytes 1310752 | tf_op jit(solution)/shard_map/all_to_all | solution.py:147
  130.5 2.1 %convolution_reduce_fusion = bf16[2,128,1024]{2,1,0:T(8,128)(2,1)S(1)} fusion(bf16[2,2,128,640]{3,2,1,0:T(8,128)(2,1)} %bitcast.91, bf16[640,1024,1,1]{1,0,3,2:T(8,128)(2,1)S(1)} %bitcast.89), kind=kOutput, calls=%fused_computation.17 | convolution fusion | flops 671350784 | bytes 2490368 | tf_op jit(solution)/shard_map/dot_general | solution.py:148
  132.7 0.8 pad_maximum_fusion.7
  (49 shorter events, 4.6 us)
Async XLA Ops:
  0.6 44.6 %copy-start = (bf16[1,384,2048]{2,1,0:T(8,128)(2,1)S(1)}, bf16[1,384,2048]{2,1,0:T(8,128)(2,1)}, u32[]{:S(2)}) copy-start(bf16[1,384,2048]{2,1,0:T(8,128)(2,1)} %param.9) | copy-start | bytes 4718596
  4.6 37.6 %copy-start.1 = (bf16[128,2048]{1,0:T(8,128)(2,1)S(1)}, bf16[128,2048]{1,0:T(8,128)(2,1)}, u32[]{:S(2)}) copy-start(bf16[128,2048]{1,0:T(8,128)(2,1)} %param.6) | copy-start | bytes 1572868
  4.6 37.6 %copy-start.4 = (bf16[2048,16]{0,1:T(8,128)(2,1)S(1)}, bf16[2048,16]{0,1:T(8,128)(2,1)}, u32[]{:S(2)}) copy-start(bf16[2048,16]{0,1:T(8,128)(2,1)} %param.7) | copy-start | bytes 196612
  4.6 37.6 %all-to-all-start = ((bf16[16,40,1024]{2,1,0:T(8,128)(2,1)}), bf16[16,40,1024]{2,1,0:T(8,128)(2,1)S(1)}, u32[]{:S(2)}, u32[]{:S(2)}) async-start(bf16[16,40,1024]{2,1,0:T(8,128)(2,1)} %bitcast.5), calls=%async_computation | async-start | bytes 2621440 | tf_op jit(solution)/shard_map/all_to_all | solution.py:89
  11.3 74.1 %collective-permute-start.7 = (bf16[384,2048]{1,0:T(8,128)(2,1)}, bf16[384,2048]{1,0:T(8,128)(2,1)}, u32[]{:S(2)}, u32[]{:S(2)}) collective-permute-start(bf16[384,2048]{1,0:T(8,128)(2,1)} %bitcast.85), channel_id=1, source_target_pairs={{0,16},{16,0},{1,17},{17,1},{2,18},{18,2},{3,19},{19,3},{4,20},{20... | collective-permute-start | bytes 4718600 | tf_op jit(solution)/shard_map/ppermute | solution.py:16
  43.8 4.4 %collective-permute-start = (f32[8,128]{1,0:T(8,128)S(1)}, f32[8,128]{1,0:T(8,128)S(1)}, u32[]{:S(2)}, u32[]{:S(2)}) collective-permute-start(f32[8,128]{1,0:T(8,128)S(1)} %broadcast_in_dim.52), channel_id=1, source_target_pairs={{0,1},{1,0},{2,3},{3,2},{4,5},{5,4},{6,7},{7,6},{8,9},{9,8},{10,11... | collective-permute-start | bytes 12296 | tf_op jit(solution)/shard_map/ppermute | solution.py:48
  45.2 2.2 %copy-start.5 = (bf16[1,384,2048]{2,1,0:T(8,128)(2,1)S(1)}, bf16[1,384,2048]{2,1,0:T(8,128)(2,1)}, u32[]{:S(2)}) copy-start(bf16[1,384,2048]{2,1,0:T(8,128)(2,1)} %param.10) | copy-start | bytes 4718596
  46.1 29.9 %collective-permute-start.4 = (bf16[16,40,1024]{2,1,0:T(8,128)(2,1)S(1)}, bf16[16,40,1024]{2,1,0:T(8,128)(2,1)S(1)}, u32[]{:S(2)}, u32[]{:S(2)}) collective-permute-start(bf16[16,40,1024]{2,1,0:T(8,128)(2,1)S(1)} %all-to-all-done), channel_id=1, source_target_pairs={{0,16},{16,0},{1,17},{17,1},{2,18},{18,2},{3,19},{19,3},{4,20},{20... | collective-permute-start | bytes 3932168 | tf_op jit(solution)/shard_map/ppermute | solution.py:16
  48.9 2.8 %collective-permute-start.1 = (f32[8,128]{1,0:T(8,128)S(1)}, f32[8,128]{1,0:T(8,128)S(1)}, u32[]{:S(2)}, u32[]{:S(2)}) collective-permute-start(f32[8,128]{1,0:T(8,128)S(1)} %broadcast_add_fusion), channel_id=1, source_target_pairs={{0,2},{1,3},{2,0},{3,1},{4,6},{5,7},{6,4},{7,5},{8,10},{9,11},{10,... | collective-permute-start | bytes 12296 | tf_op jit(solution)/shard_map/ppermute | solution.py:48
  52.4 2.8 %collective-permute-start.2 = (f32[8,128]{1,0:T(8,128)S(1)}, f32[8,128]{1,0:T(8,128)S(1)}, u32[]{:S(2)}, u32[]{:S(2)}) collective-permute-start(f32[8,128]{1,0:T(8,128)S(1)} %fusion.85), channel_id=1, source_target_pairs={{0,4},{1,5},{2,6},{3,7},{4,0},{5,1},{6,2},{7,3},{8,12},{9,13},{10,... | collective-permute-start | bytes 12296 | tf_op jit(solution)/shard_map/ppermute | solution.py:48
  55.2 3.4 %collective-permute-start.3 = (f32[8,128]{1,0:T(8,128)S(1)}, f32[8,128]{1,0:T(8,128)S(1)}, u32[]{:S(2)}, u32[]{:S(2)}) collective-permute-start(f32[8,128]{1,0:T(8,128)S(1)} %add.146), channel_id=1, source_target_pairs={{0,8},{1,9},{2,10},{3,11},{4,12},{5,13},{6,14},{7,15},{8,0},{9,1},... | collective-permute-start | bytes 12296 | tf_op jit(solution)/shard_map/ppermute | solution.py:48
  79.1 8.0 %copy-start.2 = (bf16[1,384,2048]{2,1,0:T(8,128)(2,1)S(1)}, bf16[1,384,2048]{2,1,0:T(8,128)(2,1)}, u32[]{:S(2)}) copy-start(bf16[1,384,2048]{2,1,0:T(8,128)(2,1)} %param.11) | copy-start | bytes 4718596
  79.1 6.3 %collective-permute-start.6 = (bf16[320,384]{1,0:T(8,128)(2,1)S(1)}, bf16[320,384]{1,0:T(8,128)(2,1)S(1)}, u32[]{:S(2)}, u32[]{:S(2)}) collective-permute-start(bf16[320,384]{1,0:T(8,128)(2,1)S(1)} %fusion.24), channel_id=1, source_target_pairs={{0,16},{16,0},{1,17},{17,1},{2,18},{18,2},{3,19},{19,3},{4,20},{20... | collective-permute-start | bytes 737288 | tf_op jit(solution)/shard_map/ppermute | solution.py:22
  80.3 5.0 %collective-permute-start.5 = (f32[8,128]{1,0:T(8,128)S(1)}, f32[8,128]{1,0:T(8,128)S(1)}, u32[]{:S(2)}, u32[]{:S(2)}) collective-permute-start(f32[8,128]{1,0:T(8,128)S(1)} %add.147), channel_id=1, source_target_pairs={{0,16},{16,0},{1,17},{17,1},{2,18},{18,2},{3,19},{19,3},{4,20},{20... | collective-permute-start | bytes 12296 | tf_op jit(solution)/shard_map/ppermute | solution.py:48
  89.2 1.1 copy-start.3
  92.6 37.9 %all-to-all-start.1 = ((bf16[16,40,1024]{2,1,0:T(8,128)(2,1)}), bf16[16,40,1024]{2,1,0:T(8,128)(2,1)S(1)}, u32[]{:S(2)}, u32[]{:S(2)}) async-start(bf16[16,40,1024]{2,1,0:T(8,128)(2,1)} %bitcast.90), calls=%async_computation.1 | async-start | bytes 2621440 | tf_op jit(solution)/shard_map/all_to_all | solution.py:147
